TPU v7x, 32 devices: a whole 2x2x4 slice. The times are simulated.
32 devices in a mesh: row: 4 (over y, x), col: 2 (over core), depth: 4 (over z).
Axes of the slice: x: 2, y: 2, z: 4, core: 2. Of those that a mesh axis runs over, the one named last changes fastest.
Arguments:
- a_cols: float32 [4096, 1024], P(('row', 'col')), may hold values from -16 to 24, as said below
- past_panels: float32 [4096, 2048], P(('row', 'col'), 'depth'), may hold values from -1 to 1
Outputs:
- factor: float32 [4096, 1024], P(('row', 'col'))
Inputs may be any that keep to these rules, and one draw needn't show every extreme that they name: a_cols minus past_panels times the transpose of the top 1024 rows of past_panels is the first 1024 columns of a symmetric positive definite matrix whose top block has eigenvalues between 2 and 12.
All inputs are finite; a program needn't handle non-finite values.
Results may differ from a plain program's by a relative error of at most 0.0001.
Values sent between devices are 32-bit elements.
A program may use at most 64 MiB of HBM per device.

v0:
```python
import jax
import jax.numpy as jnp
from jax import lax
from jax.sharding import PartitionSpec as P

NB = 512
STEPS = 2


def spread(array, axis, root):
    mine = lax.axis_index(axis) == root
    return lax.psum(jnp.where(mine, array, jnp.zeros_like(array)), axis)


def outer_rows(left, right):
    return lax.dot_general(
        left,
        right,
        (((1,), (1,)), ((), ())),
        precision=lax.Precision.HIGHEST,
        preferred_element_type=jnp.float32,
    )


def body(a_cols, past_panels):
    local_rows = a_cols.shape[0]
    position = lax.axis_index(("row", "col"))
    row_ids = position * local_rows + lax.broadcasted_iota(jnp.int32, (local_rows, NB), 0)
    col_ids = lax.broadcasted_iota(jnp.int32, (local_rows, NB), 1)
    result = jnp.zeros(a_cols.shape, jnp.float32)
    for section in range(STEPS):
        start = section * NB
        root = start // local_rows
        above = spread(past_panels, ("row", "col"), root)
        partial_value = outer_rows(past_panels, above)
        if section > 0:
            layer = lax.axis_index("depth")
            owned_ids = [layer + 0]
            owned_cols = [
                lax.dynamic_slice_in_dim(result, jnp.minimum(index, section - 1) * NB, NB, 1)
                for index in owned_ids
            ]
            sent_rows = jnp.stack([block for block in owned_cols])
            got_rows = spread(sent_rows, ("row", "col"), root)
            weight = (owned_ids[0] < section).astype(jnp.float32)
            partial_value = partial_value + weight * outer_rows(owned_cols[0], got_rows[0])
        summed = lax.psum(partial_value, "depth")
        update = a_cols[:, start : start + NB] - summed
        block = spread(update, ("row", "col"), root)
        diag_factor = jnp.linalg.cholesky(block)
        solved = jax.scipy.linalg.solve_triangular(diag_factor, update.T, lower=True).T
        new_panel = jnp.where(row_ids >= start + col_ids, solved, jnp.float32(0.0))
        result = result.at[:, start : start + NB].set(new_panel)
    return result


def solution(mesh):
    in_specs = (P(("row", "col"), None), P(("row", "col"), "depth"))
    out_specs = P(("row", "col"), None)
    return jax.shard_map(body, mesh=mesh, in_specs=in_specs, out_specs=out_specs, check_vma=False)
```

profile of v0, /device:TPU:0, one launch (start us, length us, event | category | flops | bytes accessed | tf_op | source)
XLA Modules:
  0.0 672.5 jit_solution(3477876616623234303)
XLA Ops:
  9.8 60.1 %all-reduce.10.cloned.1.call-done = f32[512,512]{0,1:T(8,128)} async-done(((f32[512,512]{0,1:T(8,128)}), f32[512,512]{0,1:T(8,128)}) %all-reduce.10.cloned.1.call-update) | async-done | bytes 1048592 | tf_op jit(solution)/shard_map/psum | solution.py:12
  78.8 48.2 %all-reduce.12.cloned.1.call-done = f32[512,512]{0,1:T(8,128)} async-done(((f32[512,512]{0,1:T(8,128)}), f32[512,512]{0,1:T(8,128)}) %all-reduce.12.cloned.1.call-update) | async-done | bytes 1048592 | tf_op jit(solution)/shard_map/psum | solution.py:47
  130.8 55.3 %all-reduce.14.cloned.1.call-done = f32[512,512]{0,1:T(8,128)} async-done(((f32[512,512]{0,1:T(8,128)}), f32[512,512]{0,1:T(8,128)}) %all-reduce.14.cloned.1.call-update) | async-done | bytes 1048592 | tf_op jit(solution)/shard_map/psum | solution.py:12
  189.0 11.7 %cholesky.286 = f32[128,128]{1,0:T(8,128)S(1)} custom-call(f32[128,128]{1,0:T(8,128)S(1)} %cholesky.426), custom_call_target="Cholesky" | custom-call | tf_op jit(solution)/shard_map/jit(cholesky)/cholesky | solution.py:50
  200.8 9.8 %custom-call.27 = f32[1,128,128]{1,2,0:T(8,128)S(1)} custom-call(f32[1,128,128]{2,1,0:T(8,128)S(1)} %get-tuple-element.96), custom_call_target="InvertDiagBlocksLowerTriangular" | custom-call | tf_op jit(solution)/shard_map/jit(cholesky)/cholesky | solution.py:50
  213.2 11.7 %cholesky.305 = f32[128,128]{1,0:T(8,128)S(1)} custom-call(f32[128,128]{1,0:T(8,128)S(1)} %cholesky.430), custom_call_target="Cholesky" | custom-call | tf_op jit(solution)/shard_map/jit(cholesky)/cholesky | solution.py:50
  225.0 10.3 %custom-call.28 = f32[1,128,128]{1,2,0:T(8,128)S(1)} custom-call(f32[1,128,128]{2,1,0:T(8,128)S(1)} %get-tuple-element.93), custom_call_target="InvertDiagBlocksLowerTriangular" | custom-call | tf_op jit(solution)/shard_map/jit(cholesky)/cholesky | solution.py:50
  236.9 11.7 %cholesky.326 = f32[128,128]{1,0:T(8,128)S(1)} custom-call(f32[128,128]{1,0:T(8,128)S(1)} %cholesky.435), custom_call_target="Cholesky" | custom-call | tf_op jit(solution)/shard_map/jit(cholesky)/cholesky | solution.py:50
  249.2 9.8 %custom-call.29 = f32[1,128,128]{1,2,0:T(8,128)S(1)} custom-call(f32[1,128,128]{2,1,0:T(8,128)S(1)} %get-tuple-element.90), custom_call_target="InvertDiagBlocksLowerTriangular" | custom-call | tf_op jit(solution)/shard_map/jit(cholesky)/cholesky | solution.py:50
  260.5 11.7 %cholesky.343 = f32[128,128]{1,0:T(8,128)S(1)} custom-call(f32[128,128]{1,0:T(8,128)S(1)} %convolution_subtract_fusion.11), custom_call_target="Cholesky" | custom-call | tf_op jit(solution)/shard_map/jit(cholesky)/cholesky | solution.py:50
  277.3 11.1 %while.6 = (s32[]{:T(128)}, f32[512,512]{1,0:T(8,128)}, s32[4,2]{0,1:T(2,128)S(1)}, f32[4,128,128]{2,1,0:T(8,128)S(1)}, s32[]{:T(128)}) while((s32[]{:T(128)}, f32[512,512]{1,0:T(8,128)}, s32[4,2]{0,1:T(2,128)S(1)}, f32[4,128,128]{2,1,0:T(8,128)S(1)}, s32[]{:T(128)}) %tuple.63), condition=%wide.while_cond.2, body=%wide.while_body.2.sunk | while | flops 2 | bytes 131181 | solution.py:51
  288.4 39.3 %custom-call.30 = f32[4,128,128]{1,2,0:T(8,128)S(1)} custom-call(f32[4,128,128]{2,1,0:T(8,128)S(1)} %get-tuple-element.45), custom_call_target="InvertDiagBlocksLowerTriangular" | custom-call | tf_op jit(solution)/shard_map/jit(_solve_triangular)/triangular_solve | solution.py:51
  335.6 61.2 %all-reduce.20.cloned.1.call-done = (f32[512,512]{0,1:T(8,128)}, f32[512,512]{0,1:T(8,128)}) async-done(((f32[512,512]{0,1:T(8,128)}, f32[512,512]{0,1:T(8,128)}), (f32[512,512]{0,1:T(8,128)}, f32[512,512]{0,1:T(8,128)})) %all-reduce.20.cloned.1.call-update) | async-done | bytes 2097168 | tf_op jit(solution)/shard_map/psum | solution.py:12
  405.1 50.5 %all-reduce.16.cloned.1.call-done = f32[512,512]{0,1:T(8,128)} async-done(((f32[512,512]{0,1:T(8,128)}), f32[512,512]{0,1:T(8,128)}) %all-reduce.16.cloned.1.call-update) | async-done | bytes 1048592 | tf_op jit(solution)/shard_map/psum | solution.py:47
  458.4 56.2 %all-reduce.18.cloned.1.call-done = f32[512,512]{0,1:T(8,128)} async-done(((f32[512,512]{0,1:T(8,128)}), f32[512,512]{0,1:T(8,128)}) %all-reduce.18.cloned.1.call-update) | async-done | bytes 1048592 | tf_op jit(solution)/shard_map/psum | solution.py:12
  517.5 11.7 %cholesky.358 = f32[128,128]{1,0:T(8,128)S(1)} custom-call(f32[128,128]{1,0:T(8,128)S(1)} %cholesky.439), custom_call_target="Cholesky" | custom-call | tf_op jit(solution)/shard_map/jit(cholesky)/cholesky | solution.py:50
  529.4 9.8 %custom-call.31 = f32[1,128,128]{1,2,0:T(8,128)S(1)} custom-call(f32[1,128,128]{2,1,0:T(8,128)S(1)} %get-tuple-element.86), custom_call_target="InvertDiagBlocksLowerTriangular" | custom-call | tf_op jit(solution)/shard_map/jit(cholesky)/cholesky | solution.py:50
  541.7 11.7 %cholesky.377 = f32[128,128]{1,0:T(8,128)S(1)} custom-call(f32[128,128]{1,0:T(8,128)S(1)} %cholesky.443), custom_call_target="Cholesky" | custom-call | tf_op jit(solution)/shard_map/jit(cholesky)/cholesky | solution.py:50
  554.8 10.2 %custom-call.32 = f32[1,128,128]{1,2,0:T(8,128)S(1)} custom-call(f32[1,128,128]{2,1,0:T(8,128)S(1)} %get-tuple-element.83), custom_call_target="InvertDiagBlocksLowerTriangular" | custom-call | tf_op jit(solution)/shard_map/jit(cholesky)/cholesky | solution.py:50
  566.6 11.7 %cholesky.398 = f32[128,128]{1,0:T(8,128)S(1)} custom-call(f32[128,128]{1,0:T(8,128)S(1)} %cholesky.448), custom_call_target="Cholesky" | custom-call | tf_op jit(solution)/shard_map/jit(cholesky)/cholesky | solution.py:50
  579.0 9.8 %custom-call.33 = f32[1,128,128]{1,2,0:T(8,128)S(1)} custom-call(f32[1,128,128]{2,1,0:T(8,128)S(1)} %get-tuple-element.80), custom_call_target="InvertDiagBlocksLowerTriangular" | custom-call | tf_op jit(solution)/shard_map/jit(cholesky)/cholesky | solution.py:50
  590.3 11.8 %cholesky.415 = f32[128,128]{1,0:T(8,128)S(1)} custom-call(f32[128,128]{1,0:T(8,128)S(1)} %convolution_subtract_fusion.10), custom_call_target="Cholesky" | custom-call | tf_op jit(solution)/shard_map/jit(cholesky)/cholesky | solution.py:50
  606.4 11.7 %while.7 = (s32[]{:T(128)}, f32[512,512]{1,0:T(8,128)}, s32[4,2]{0,1:T(2,128)S(1)}, f32[4,128,128]{2,1,0:T(8,128)S(1)}, s32[]{:T(128)}) while((s32[]{:T(128)}, f32[512,512]{1,0:T(8,128)}, s32[4,2]{0,1:T(2,128)S(1)}, f32[4,128,128]{2,1,0:T(8,128)S(1)}, s32[]{:T(128)}) %tuple.82), condition=%wide.while_cond.2.clone, body=%wide.while_body.2.clone.sunk | while | flops 2 | bytes 131181 | solution.py:51
  618.1 39.3 %custom-call.34 = f32[4,128,128]{1,2,0:T(8,128)S(1)} custom-call(f32[4,128,128]{2,1,0:T(8,128)S(1)} %get-tuple-element.46), custom_call_target="InvertDiagBlocksLowerTriangular" | custom-call | tf_op jit(solution)/shard_map/jit(_solve_triangular)/triangular_solve | solution.py:51
  (131 shorter events, 89.5 us)
Async XLA Ops:
  6.5 63.4 %all-reduce.10.cloned.1.call-start = ((), (), s32[]{:S(2)}) async-start(), calls=%async_computation | async-start | bytes 2097152 | tf_op jit(solution)/shard_map/psum | solution.py:12
  8.1 61.8 %copy-start = (f32[512,512]{1,0:T(8,128)S(1)}, f32[512,512]{1,0:T(8,128)}, u32[]{:S(2)}) copy-start(f32[512,512]{1,0:T(8,128)} %param.10) | copy-start | bytes 3145732
  9.8 117.2 %all-reduce.12.cloned.1.call-start = ((), (), s32[]{:S(2)}) async-start(), calls=%async_computation.1 | async-start | bytes 2097152 | tf_op jit(solution)/shard_map/psum | solution.py:47
  75.7 110.4 %all-reduce.14.cloned.1.call-start = ((), (), s32[]{:S(2)}) async-start(), calls=%async_computation.2 | async-start | bytes 2097152 | tf_op jit(solution)/shard_map/psum | solution.py:12
  129.8 267.0 %all-reduce.20.cloned.1.call-start = ((), (), s32[]{:S(2)}) async-start(), calls=%async_computation.5 | async-start | bytes 4194304 | tf_op jit(solution)/shard_map/psum | solution.py:12
  186.1 1.7 copy-start.1
  188.0 1.0 copy-start.7
  236.9 90.9 %copy-start.3 = (f32[512,512]{1,0:T(8,128)S(1)}, f32[512,512]{1,0:T(8,128)}, u32[]{:S(2)}) copy-start(f32[512,512]{1,0:T(8,128)} %get-tuple-element.72) | copy-start | bytes 3145732
  335.5 120.1 %all-reduce.16.cloned.1.call-start = ((), (), s32[]{:S(2)}) async-start(), calls=%async_computation.3 | async-start | bytes 2097152 | tf_op jit(solution)/shard_map/psum | solution.py:47
  396.8 4.8 copy-start.8
  401.6 3.2 copy-start.5
  404.5 110.1 %all-reduce.18.cloned.1.call-start = ((), (), s32[]{:S(2)}) async-start(), calls=%async_computation.4 | async-start | bytes 2097152 | tf_op jit(solution)/shard_map/psum | solution.py:12
  514.6 1.7 copy-start.2
  516.5 1.0 copy-start.6
  566.6 90.9 %copy-start.4 = (f32[512,512]{1,0:T(8,128)S(1)}, f32[512,512]{1,0:T(8,128)}, u32[]{:S(2)}) copy-start(f32[512,512]{1,0:T(8,128)} %get-tuple-element.70) | copy-start | bytes 3145732
Sparse Core Ops, SparseCore 0:
  10.5 59.4 all-reduce.9
  75.8 51.1 all-reduce.11
  130.1 55.9 all-reduce.13
  335.6 61.0 all-reduce.19
  404.6 50.9 all-reduce.15
  458.6 55.9 all-reduce.17
where the time goes:
time: 678 us; the launch traced here: 672 us
  waiting for transfers between devices  332 us (49%)
  other arithmetic  250 us (37%)
  matrix products  35.9 us (5%)
  local copies, waits for them, and re-layouts  34.9 us (5%)
  between operations  19.2 us (3%)
    psum x4, waiting for transfers between devices, spread(): return lax.psum(jnp.where(mine, array, jnp.zeros_like(array)), axis)  233 us
    another operation x29, other arithmetic, body(): diag_factor = jnp.linalg.cholesky(block)  158 us
    psum x2, waiting for transfers between devices, body(): summed = lax.psum(partial_value, 'depth')  98.7 us
    another operation x5, other arithmetic, body(): jax.scipy.linalg.solve_triangular(diag_factor, update.T, lower=True)  81 us
    another operation x27, local copies, waits for them, and re-layouts, body(): jax.scipy.linalg.solve_triangular(diag_factor, update.T, lower=True)  22.6 us
  transfers between devices with their start and end apart: 6, of which 6 were waited for; matrix products, arithmetic and copies ran while one was open for 1% of the time, Pallas kernels for 0%

commit v1 on v0

--- a/solution.py
+++ b/solution.py
@@ -1,3 +1,4 @@
+import functools
 import jax
 import jax.numpy as jnp
 from jax import lax
@@ -5,6 +6,18 @@
 
 NB = 512
 STEPS = 2
+
+
+def area_rest(work_x, mesh_ax):
+    world = jax.lax.axis_size(mesh_ax)
+    h_now = work_x
+    for dev_j in [[(it, it ^ kk) for it in range(world)] for kk in (1, 2, 4, 8, 16) if kk < world]:
+        base_arr = jax.lax.ppermute(h_now, mesh_ax, dev_j)
+        h_now = h_now + base_arr
+    return h_now
+
+
+obtain_tiles_all = functools.partial(area_rest, mesh_ax="depth")
 
 
 def spread(array, axis, root):
@@ -44,7 +57,7 @@
             got_rows = spread(sent_rows, ("row", "col"), root)
             weight = (owned_ids[0] < section).astype(jnp.float32)
             partial_value = partial_value + weight * outer_rows(owned_cols[0], got_rows[0])
-        summed = lax.psum(partial_value, "depth")
+        summed = obtain_tiles_all(partial_value)
         update = a_cols[:, start : start + NB] - summed
         block = spread(update, ("row", "col"), root)
         diag_factor = jnp.linalg.cholesky(block)

time: 678 us -> 717 us (1.058)
  waiting for transfers between devices: 332 us -> 363 us
  starting transfers between devices: 0.42 us -> 8.02 us
    ppermute x0 -> x4, waiting for transfers between devices: none -> 129 us  [area_rest(): base_arr = jax.lax.ppermute(h_now, mesh_ax, dev_j)]
    psum x2 -> x0, waiting for transfers between devices: 98.7 us -> none  [body(): summed = lax.psum(partial_value, 'depth')]
    ppermute x0 -> x4, starting transfers between devices: none -> 7.89 us  [area_rest(): base_arr = jax.lax.ppermute(h_now, mesh_ax, dev_j)]
  transfers between devices with their start and end apart: 6 -> 8, of which waited for: 6 -> 8; matrix products, arithmetic and copies ran while one was open for 1% -> 1% of each run, Pallas kernels for 0% -> 0%
where the time goes in v1:
time: 717 us; the launch traced here: 711 us
  waiting for transfers between devices  363 us (51%)
  other arithmetic  251 us (35%)
  local copies, waits for them, and re-layouts  35.9 us (5%)
  matrix products  33.9 us (5%)
  between operations  19 us (3%)
  starting transfers between devices  8.02 us (1%)
    psum x4, waiting for transfers between devices, spread(): return lax.psum(jnp.where(mine, array, jnp.zeros_like(array)), axis)  234 us
    another operation x29, other arithmetic, body(): diag_factor = jnp.linalg.cholesky(block)  158 us
    ppermute x4, waiting for transfers between devices, area_rest(): base_arr = jax.lax.ppermute(h_now, mesh_ax, dev_j)  129 us
    another operation x5, other arithmetic, body(): jax.scipy.linalg.solve_triangular(diag_factor, update.T, lower=True)  81.2 us
    another operation x27, local copies, waits for them, and re-layouts, body(): jax.scipy.linalg.solve_triangular(diag_factor, update.T, lower=True)  22.6 us
  transfers between devices with their start and end apart: 8, of which 8 were waited for; matrix products, arithmetic and copies ran while one was open for 1% of the time, Pallas kernels for 0%

profile of v1, /device:TPU:0, one launch (start us, length us, event | category | flops | bytes accessed | tf_op | source)
XLA Modules:
  0.0 711.5 jit_solution(1821003272218856243)
XLA Ops:
  9.9 60.1 %all-reduce.8.cloned.1.call-done = f32[512,512]{0,1:T(8,128)} async-done(((f32[512,512]{0,1:T(8,128)}), f32[512,512]{0,1:T(8,128)}) %all-reduce.8.cloned.1.call-update) | async-done | bytes 1048592 | tf_op jit(solution)/shard_map/psum | solution.py:25
  76.1 22.6 %collective-permute-done = f32[512,512]{0,1:T(8,128)S(1)} collective-permute-done((f32[512,512]{0,1:T(8,128)S(1)}, f32[512,512]{0,1:T(8,128)S(1)}, u32[]{:S(2)}, u32[]{:S(2)}) %collective-permute-start) | collective-permute-done | bytes 1048608 | tf_op jit(solution)/shard_map/ppermute | solution.py:15
  104.5 41.1 %collective-permute-done.1 = f32[512,512]{0,1:T(8,128)} collective-permute-done((f32[512,512]{0,1:T(8,128)S(1)}, f32[512,512]{0,1:T(8,128)}, u32[]{:S(2)}, u32[]{:S(2)}) %collective-permute-start.1) | collective-permute-done | bytes 1048608 | tf_op jit(solution)/shard_map/ppermute | solution.py:15
  149.8 55.3 %all-reduce.10.cloned.1.call-done = f32[512,512]{0,1:T(8,128)} async-done(((f32[512,512]{0,1:T(8,128)}), f32[512,512]{0,1:T(8,128)}) %all-reduce.10.cloned.1.call-update) | async-done | bytes 1048592 | tf_op jit(solution)/shard_map/psum | solution.py:25
  208.0 11.7 %cholesky.286 = f32[128,128]{1,0:T(8,128)S(1)} custom-call(f32[128,128]{1,0:T(8,128)S(1)} %cholesky.426), custom_call_target="Cholesky" | custom-call | tf_op jit(solution)/shard_map/jit(cholesky)/cholesky | solution.py:63
  219.9 9.8 %custom-call.27 = f32[1,128,128]{1,2,0:T(8,128)S(1)} custom-call(f32[1,128,128]{2,1,0:T(8,128)S(1)} %get-tuple-element.96), custom_call_target="InvertDiagBlocksLowerTriangular" | custom-call | tf_op jit(solution)/shard_map/jit(cholesky)/cholesky | solution.py:63
  232.2 11.7 %cholesky.305 = f32[128,128]{1,0:T(8,128)S(1)} custom-call(f32[128,128]{1,0:T(8,128)S(1)} %cholesky.430), custom_call_target="Cholesky" | custom-call | tf_op jit(solution)/shard_map/jit(cholesky)/cholesky | solution.py:63
  244.0 10.0 %custom-call.28 = f32[1,128,128]{1,2,0:T(8,128)S(1)} custom-call(f32[1,128,128]{2,1,0:T(8,128)S(1)} %get-tuple-element.93), custom_call_target="InvertDiagBlocksLowerTriangular" | custom-call | tf_op jit(solution)/shard_map/jit(cholesky)/cholesky | solution.py:63
  255.5 11.7 %cholesky.326 = f32[128,128]{1,0:T(8,128)S(1)} custom-call(f32[128,128]{1,0:T(8,128)S(1)} %cholesky.435), custom_call_target="Cholesky" | custom-call | tf_op jit(solution)/shard_map/jit(cholesky)/cholesky | solution.py:63
  279.1 11.7 %cholesky.343 = f32[128,128]{1,0:T(8,128)S(1)} custom-call(f32[128,128]{1,0:T(8,128)S(1)} %convolution_subtract_fusion.5), custom_call_target="Cholesky" | custom-call | tf_op jit(solution)/shard_map/jit(cholesky)/cholesky | solution.py:63
  296.3 11.1 %while.6 = (s32[]{:T(128)}, f32[512,512]{1,0:T(8,128)}, s32[4,2]{0,1:T(2,128)S(1)}, f32[4,128,128]{2,1,0:T(8,128)S(1)}, s32[]{:T(128)}) while((s32[]{:T(128)}, f32[512,512]{1,0:T(8,128)}, s32[4,2]{0,1:T(2,128)S(1)}, f32[4,128,128]{2,1,0:T(8,128)S(1)}, s32[]{:T(128)}) %tuple.63), condition=%wide.while_cond.2, body=%wide.while_body.2.sunk | while | flops 2 | bytes 131181 | solution.py:64
  307.4 39.3 %custom-call.30 = f32[4,128,128]{1,2,0:T(8,128)S(1)} custom-call(f32[4,128,128]{2,1,0:T(8,128)S(1)} %get-tuple-element.45), custom_call_target="InvertDiagBlocksLowerTriangular" | custom-call | tf_op jit(solution)/shard_map/jit(_solve_triangular)/triangular_solve | solution.py:64
  354.5 61.2 %all-reduce.14.cloned.1.call-done = (f32[512,512]{0,1:T(8,128)}, f32[512,512]{0,1:T(8,128)}) async-done(((f32[512,512]{0,1:T(8,128)}, f32[512,512]{0,1:T(8,128)}), (f32[512,512]{0,1:T(8,128)}, f32[512,512]{0,1:T(8,128)})) %all-reduce.14.cloned.1.call-update) | async-done | bytes 2097168 | tf_op jit(solution)/shard_map/psum | solution.py:25
  423.9 22.3 %collective-permute-done.2 = f32[512,512]{0,1:T(8,128)S(1)} collective-permute-done((f32[512,512]{0,1:T(8,128)S(1)}, f32[512,512]{0,1:T(8,128)S(1)}, u32[]{:S(2)}, u32[]{:S(2)}) %collective-permute-start.2) | collective-permute-done | bytes 1048608 | tf_op jit(solution)/shard_map/ppermute | solution.py:15
  450.3 42.6 %collective-permute-done.3 = f32[512,512]{0,1:T(8,128)} collective-permute-done((f32[512,512]{0,1:T(8,128)S(1)}, f32[512,512]{0,1:T(8,128)}, u32[]{:S(2)}, u32[]{:S(2)}) %collective-permute-start.3) | collective-permute-done | bytes 1048608 | tf_op jit(solution)/shard_map/ppermute | solution.py:15
  496.2 57.9 %all-reduce.12.cloned.1.call-done = f32[512,512]{0,1:T(8,128)} async-done(((f32[512,512]{0,1:T(8,128)}), f32[512,512]{0,1:T(8,128)}) %all-reduce.12.cloned.1.call-update) | async-done | bytes 1048592 | tf_op jit(solution)/shard_map/psum | solution.py:25
  556.9 11.7 %cholesky.358 = f32[128,128]{1,0:T(8,128)S(1)} custom-call(f32[128,128]{1,0:T(8,128)S(1)} %cholesky.439), custom_call_target="Cholesky" | custom-call | tf_op jit(solution)/shard_map/jit(cholesky)/cholesky | solution.py:63
  568.8 10.0 %custom-call.31 = f32[1,128,128]{1,2,0:T(8,128)S(1)} custom-call(f32[1,128,128]{2,1,0:T(8,128)S(1)} %get-tuple-element.86), custom_call_target="InvertDiagBlocksLowerTriangular" | custom-call | tf_op jit(solution)/shard_map/jit(cholesky)/cholesky | solution.py:63
  581.3 11.7 %cholesky.377 = f32[128,128]{1,0:T(8,128)S(1)} custom-call(f32[128,128]{1,0:T(8,128)S(1)} %cholesky.443), custom_call_target="Cholesky" | custom-call | tf_op jit(solution)/shard_map/jit(cholesky)/cholesky | solution.py:63
  605.8 11.7 %cholesky.398 = f32[128,128]{1,0:T(8,128)S(1)} custom-call(f32[128,128]{1,0:T(8,128)S(1)} %cholesky.448), custom_call_target="Cholesky" | custom-call | tf_op jit(solution)/shard_map/jit(cholesky)/cholesky | solution.py:63
  618.2 10.0 %custom-call.33 = f32[1,128,128]{1,2,0:T(8,128)S(1)} custom-call(f32[1,128,128]{2,1,0:T(8,128)S(1)} %get-tuple-element.80), custom_call_target="InvertDiagBlocksLowerTriangular" | custom-call | tf_op jit(solution)/shard_map/jit(cholesky)/cholesky | solution.py:63
  629.7 11.7 %cholesky.415 = f32[128,128]{1,0:T(8,128)S(1)} custom-call(f32[128,128]{1,0:T(8,128)S(1)} %convolution_subtract_fusion.4), custom_call_target="Cholesky" | custom-call | tf_op jit(solution)/shard_map/jit(cholesky)/cholesky | solution.py:63
  645.7 11.7 %while.7 = (s32[]{:T(128)}, f32[512,512]{1,0:T(8,128)}, s32[4,2]{0,1:T(2,128)S(1)}, f32[4,128,128]{2,1,0:T(8,128)S(1)}, s32[]{:T(128)}) while((s32[]{:T(128)}, f32[512,512]{1,0:T(8,128)}, s32[4,2]{0,1:T(2,128)S(1)}, f32[4,128,128]{2,1,0:T(8,128)S(1)}, s32[]{:T(128)}) %tuple.78), condition=%wide.while_cond.2.clone, body=%wide.while_body.2.clone.sunk | while | flops 2 | bytes 131181 | solution.py:64
  657.4 39.3 %custom-call.34 = f32[4,128,128]{1,2,0:T(8,128)S(1)} custom-call(f32[4,128,128]{2,1,0:T(8,128)S(1)} %get-tuple-element.46), custom_call_target="InvertDiagBlocksLowerTriangular" | custom-call | tf_op jit(solution)/shard_map/jit(_solve_triangular)/triangular_solve | solution.py:64
  (137 shorter events, 117.2 us)
Async XLA Ops:
  6.5 63.4 %all-reduce.8.cloned.1.call-start = ((), (), s32[]{:S(2)}) async-start(), calls=%async_computation | async-start | bytes 2097152 | tf_op jit(solution)/shard_map/psum | solution.py:25
  8.1 61.8 %copy-start = (f32[512,512]{1,0:T(8,128)S(1)}, f32[512,512]{1,0:T(8,128)}, u32[]{:S(2)}) copy-start(f32[512,512]{1,0:T(8,128)} %param.10) | copy-start | bytes 3145732
  9.8 195.3 %all-reduce.10.cloned.1.call-start = ((), (), s32[]{:S(2)}) async-start(), calls=%async_computation.1 | async-start | bytes 2097152 | tf_op jit(solution)/shard_map/psum | solution.py:25
  74.6 26.8 %copy-start.8 = (f32[512,1024]{1,0:T(8,128)S(1)}, f32[512,1024]{1,0:T(8,128)}, u32[]{:S(2)}) copy-start(f32[512,1024]{1,0:T(8,128)} %param.9) | copy-start | bytes 6291460
  74.7 24.1 %collective-permute-start = (f32[512,512]{0,1:T(8,128)S(1)}, f32[512,512]{0,1:T(8,128)S(1)}, u32[]{:S(2)}, u32[]{:S(2)}) collective-permute-start(f32[512,512]{0,1:T(8,128)S(1)} %convolution_bitcast_fusion.1), channel_id=1, source_target_pairs={{0,1},{1,0},{2,3},{3,2},{4,5},{5,4},{6,7},{7,6},{8,9},{9,8},{10,11... | collective-permute-start | bytes 3145736 | tf_op jit(solution)/shard_map/ppermute | solution.py:15
  99.0 46.7 %collective-permute-start.1 = (f32[512,512]{0,1:T(8,128)S(1)}, f32[512,512]{0,1:T(8,128)}, u32[]{:S(2)}, u32[]{:S(2)}) collective-permute-start(f32[512,512]{0,1:T(8,128)S(1)} %add.91), channel_id=1, source_target_pairs={{0,2},{1,3},{2,0},{3,1},{4,6},{5,7},{6,4},{7,5},{8,10},{9,11},{10,... | collective-permute-start | bytes 3145736 | tf_op jit(solution)/shard_map/ppermute | solution.py:15
  148.6 267.1 %all-reduce.14.cloned.1.call-start = ((), (), s32[]{:S(2)}) async-start(), calls=%async_computation.3 | async-start | bytes 4194304 | tf_op jit(solution)/shard_map/psum | solution.py:25
  205.1 1.7 copy-start.1
  207.0 1.0 copy-start.7
  255.5 91.2 %copy-start.3 = (f32[512,512]{1,0:T(8,128)S(1)}, f32[512,512]{1,0:T(8,128)}, u32[]{:S(2)}) copy-start(f32[512,512]{1,0:T(8,128)} %get-tuple-element.72) | copy-start | bytes 3145732
  354.5 199.6 %all-reduce.12.cloned.1.call-start = ((), (), s32[]{:S(2)}) async-start(), calls=%async_computation.2 | async-start | bytes 2097152 | tf_op jit(solution)/shard_map/psum | solution.py:25
  415.7 4.8 copy-start.9
  422.5 26.5 %copy-start.5 = (f32[512,512]{1,0:T(8,128)S(1)}, f32[512,512]{1,0:T(8,128)}, u32[]{:S(2)}) copy-start(f32[512,512]{1,0:T(8,128)} %get-tuple-element.74) | copy-start | bytes 3145732
  422.5 23.8 %collective-permute-start.2 = (f32[512,512]{0,1:T(8,128)S(1)}, f32[512,512]{0,1:T(8,128)S(1)}, u32[]{:S(2)}, u32[]{:S(2)}) collective-permute-start(f32[512,512]{0,1:T(8,128)S(1)} %fusion), channel_id=1, source_target_pairs={{0,1},{1,0},{2,3},{3,2},{4,5},{5,4},{6,7},{7,6},{8,9},{9,8},{10,11... | collective-permute-start | bytes 3145736 | tf_op jit(solution)/shard_map/ppermute | solution.py:15
  446.5 46.4 %collective-permute-start.3 = (f32[512,512]{0,1:T(8,128)S(1)}, f32[512,512]{0,1:T(8,128)}, u32[]{:S(2)}, u32[]{:S(2)}) collective-permute-start(f32[512,512]{0,1:T(8,128)S(1)} %add.97), channel_id=1, source_target_pairs={{0,2},{1,3},{2,0},{3,1},{4,6},{5,7},{6,4},{7,5},{8,10},{9,11},{10,... | collective-permute-start | bytes 3145736 | tf_op jit(solution)/shard_map/ppermute | solution.py:15
  554.1 1.7 copy-start.2
  556.0 1.0 copy-start.6
  605.8 91.0 %copy-start.4 = (f32[512,512]{1,0:T(8,128)S(1)}, f32[512,512]{1,0:T(8,128)}, u32[]{:S(2)}) copy-start(f32[512,512]{1,0:T(8,128)} %get-tuple-element.70) | copy-start | bytes 3145732
Sparse Core Ops, SparseCore 0:
  10.5 59.4 all-reduce.7
  148.7 56.3 all-reduce.9
  354.6 61.0 all-reduce.13
  496.3 57.7 all-reduce.11
